TPU v7x, 32 devices: a whole 2x2x4 slice. The times are simulated.
32 devices in a mesh: wide: 8 (over y, x, core), narrow: 4 (over z).
Axes of the slice: x: 2, y: 2, z: 4, core: 2. Of those that a mesh axis runs over, the one named last changes fastest.
Arguments:
- layer_input: bfloat16 [4, 2048, 2048], P(None, 'wide'), may hold values from -6 to 6
- grad_out: bfloat16 [4, 2048, 2048], P(None, 'wide'), may hold values from -6 to 6
- lengths: int32 [4, 8], replicated, may hold values from 1 to 1024, 2048 in all within a row
- w_query: bfloat16 [2048, 2048], P('wide', 'narrow'), may hold values from -0.125 to 0.125
- w_key: bfloat16 [2048, 1024], P('wide', 'narrow'), may hold values from -0.125 to 0.125
- w_value: bfloat16 [2048, 1024], P('wide', 'narrow'), may hold values from -0.125 to 0.125
- w_out: bfloat16 [2048, 2048], P('narrow', 'wide'), may hold values from -0.75 to 0.75
- w_gate: bfloat16 [2048, 6144], P('wide', 'narrow'), may hold values from -0.125 to 0.125
- w_up: bfloat16 [2048, 6144], P('wide', 'narrow'), may hold values from -0.125 to 0.125
- w_down: bfloat16 [6144, 2048], P('narrow', 'wide'), may hold values from -0.078125 to 0.078125
- gain_attn: float32 [2048], replicated, may hold values from 0.25 to 1.75
- gain_ffn: float32 [2048], replicated, may hold values from 0.25 to 1.75
- gain_query: float32 [128], replicated, may hold values from 0.25 to 1.75
- gain_key: float32 [128], replicated, may hold values from 0.25 to 1.75
Outputs:
- output: bfloat16 [4, 2048, 2048], P(None, 'wide')
- grad_input: float32 [4, 2048, 2048], P(None, 'wide')
- grad_wquery: float32 [2048, 2048], P('wide', 'narrow')
- grad_wkey: float32 [2048, 1024], P('wide', 'narrow')
- grad_wvalue: float32 [2048, 1024], P('wide', 'narrow')
- grad_wout: float32 [2048, 2048], P('narrow', 'wide')
- grad_wgate: float32 [2048, 6144], P('wide', 'narrow')
- grad_wup: float32 [2048, 6144], P('wide', 'narrow')
- grad_wdown: float32 [6144, 2048], P('narrow', 'wide')
- grad_gattn: float32 [2048], replicated
- grad_gffn: float32 [2048], replicated
- grad_gquery: float32 [128], replicated
- grad_gkey: float32 [128], replicated
Inputs may be any that keep to these rules, and one draw needn't show every extreme that they name: `lengths`: each row cuts the 2048 tokens of its micro-batch into 8 consecutive pieces in order; pieces 0 to 6 are documents and the last piece is padding. A row's pieces sum to 2048, and its largest piece is exactly 1024.
All inputs are finite; a program needn't handle non-finite values.
Results may differ from a plain program's by a relative error of at most 0.022.
Values may be sent and summed in bfloat16 or wider, within the bound.
A program may use at most 256 MiB of HBM per device.

v0:
```python
import math

import jax
import jax.numpy as jnp
from jax import lax
from jax.sharding import PartitionSpec as P

HD = 128
NDOC = 8


EPSILON = 1e-06
THETA = 1000000.0


def rms_norm(values, gain):
    return values * lax.rsqrt(jnp.mean(values * values, axis=-1, keepdims=True) + EPSILON) * gain


def unit_rows(values):
    return values * lax.rsqrt(jnp.mean(values * values, axis=-1, keepdims=True) + EPSILON)


def rotate(values, cosine, sine):
    midway = values.shape[-1] // 2
    turned = jnp.concatenate([-values[..., midway:], values[..., :midway]], axis=-1)
    return values * cosine + turned * sine


def layout(lengths_row, total):
    finish = jnp.cumsum(lengths_row)
    starts = finish - lengths_row
    places = jnp.arange(total, dtype=jnp.int32)
    segment = jnp.sum((places[:, None] >= finish[None, :]).astype(jnp.int32), axis=1)
    member = segment[:, None] == jnp.arange(finish.shape[0], dtype=jnp.int32)[None, :]
    opening = jnp.sum(jnp.where(member, starts[None, :], 0), axis=1)
    return (segment, places - opening)


def angles(place):
    frequency = jnp.exp(-math.log(THETA) * jnp.arange(0, HD, 2).astype(jnp.float32) / HD)
    turning = place.astype(jnp.float32)[:, None] * frequency[None, :]
    turning = jnp.concatenate([turning, turning], axis=-1)
    return (jnp.cos(turning), jnp.sin(turning))


def allowed(query_seg, query_idx, key_seg, key_idx):
    same_doc = query_seg[:, None] == key_seg[None, :]
    causal = key_idx[None, :] <= query_idx[:, None]
    usable = (key_seg[None, :] != NDOC - 1) | (key_idx[None, :] == query_idx[:, None])
    return same_doc & causal & usable


def attention_scores(query_low, key_all, mask_local, factor):
    scores = (
        jnp.einsum("tgrd,kgd->grtk", query_low, key_all, preferred_element_type=jnp.float32)
        * factor
    )
    return jnp.where(mask_local[None, None], scores, -1e30)


def one_batch(row_input, grad_row, lengths_row, gathered, gains):
    w_query, w_key, w_value, w_out, w_gate, w_up, w_down = gathered
    gain_attn, gain_ffn, gain_query, gain_key = gains
    tok_rows = row_input.shape[0]
    total = tok_rows * lax.axis_size("wide")
    groups = w_key.shape[1] // HD
    repeat = w_query.shape[1] // w_key.shape[1]
    factor = 1.0 / math.sqrt(HD)
    first_row = lax.axis_index("wide") * tok_rows
    segment, place = layout(lengths_row, total)
    positions = jnp.arange(total, dtype=jnp.int32)
    query_seg = lax.dynamic_slice_in_dim(segment, first_row, tok_rows)
    query_idx = lax.dynamic_slice_in_dim(positions, first_row, tok_rows)
    mask_local = allowed(query_seg, query_idx, segment, positions)
    cosine, sine = angles(lax.dynamic_slice_in_dim(place, first_row, tok_rows))

    def head_norm(rows, gain):
        return rotate(rms_norm(rows, gain), cosine[:, None, :], sine[:, None, :])

    input_float = row_input.astype(jnp.float32)
    grad_float = grad_row.astype(jnp.float32)
    normed_one, pull_one = jax.vjp(lambda rows: rms_norm(rows, gain_attn), input_float)
    hidden_one = normed_one.astype(jnp.bfloat16)
    query_raw = jnp.dot(hidden_one, w_query, preferred_element_type=jnp.float32).reshape(
        tok_rows, groups * repeat, HD
    )
    key_raw = jnp.dot(hidden_one, w_key, preferred_element_type=jnp.float32).reshape(
        tok_rows, groups, HD
    )
    value_low = jnp.dot(hidden_one, w_value, preferred_element_type=jnp.float32).astype(
        jnp.bfloat16
    )
    query_turned, pull_query = jax.vjp(head_norm, query_raw, gain_query)
    key_turned, pull_key = jax.vjp(head_norm, key_raw, gain_key)
    query_low = query_turned.astype(jnp.bfloat16).reshape(tok_rows, groups, repeat, HD)
    key_low = key_turned.astype(jnp.bfloat16).reshape(tok_rows, groups * HD)
    key_all, value_all = (
        lax.all_gather(key_low, "wide", axis=0, tiled=True),
        lax.all_gather(value_low, "wide", axis=0, tiled=True),
    )
    key_all = key_all.reshape(total, groups, HD)
    value_all = value_all.reshape(total, groups, HD)
    scores = attention_scores(query_low, key_all, mask_local, factor)
    highest = jnp.max(scores, axis=-1, keepdims=True)
    exponent = jnp.exp(scores - highest)
    denominator = jnp.sum(exponent, axis=-1, keepdims=True)
    log_total = highest + jnp.log(denominator)
    probs_low = (exponent / denominator).astype(jnp.bfloat16)
    mixed = jnp.einsum("grtk,kgd->tgrd", probs_low, value_all, preferred_element_type=jnp.float32)
    mixed_low = mixed.reshape(tok_rows, groups * repeat * HD).astype(jnp.bfloat16)
    attn_part = jnp.dot(mixed_low, w_out, preferred_element_type=jnp.float32)
    middle = input_float + lax.psum(attn_part.astype(jnp.bfloat16), "narrow").astype(jnp.float32)
    normed_two, pull_two = jax.vjp(lambda rows: rms_norm(rows, gain_ffn), middle)
    hidden_two = normed_two.astype(jnp.bfloat16)
    unit_two = unit_rows(middle)
    gate = jnp.dot(hidden_two, w_gate, preferred_element_type=jnp.float32)
    up_proj = jnp.dot(hidden_two, w_up, preferred_element_type=jnp.float32)
    active, pull_active = jax.vjp(
        lambda gate_in, up_in: jax.nn.silu(gate_in) * up_in, gate, up_proj
    )
    active_low = active.astype(jnp.bfloat16)
    ffn_part = jnp.dot(active_low, w_down, preferred_element_type=jnp.float32)
    output_low = (
        middle + lax.psum(ffn_part.astype(jnp.bfloat16), "narrow").astype(jnp.float32)
    ).astype(jnp.bfloat16)
    grad_wdown = jnp.einsum("tf,td->fd", active_low, grad_row, preferred_element_type=jnp.float32)
    grad_active = jnp.einsum("td,fd->tf", grad_row, w_down, preferred_element_type=jnp.float32)
    grad_gate, grad_upper = pull_active(grad_active)
    gate_back = grad_gate.astype(jnp.bfloat16)
    upper_back = grad_upper.astype(jnp.bfloat16)
    grad_wgate = jnp.einsum("td,tf->df", hidden_two, gate_back, preferred_element_type=jnp.float32)
    grad_wup = jnp.einsum("td,tf->df", hidden_two, upper_back, preferred_element_type=jnp.float32)
    partial_two = jnp.einsum(
        "tf,df->td", gate_back, w_gate, preferred_element_type=jnp.float32
    ) + jnp.einsum("tf,df->td", upper_back, w_up, preferred_element_type=jnp.float32)
    gain_two = jnp.sum(partial_two * unit_two, axis=0)
    grad_middle = (
        grad_float
        + pull_two(lax.psum(partial_two.astype(jnp.bfloat16), "narrow").astype(jnp.float32))[0]
    )
    middle_low = grad_middle.astype(jnp.bfloat16)
    grad_wout = jnp.einsum("th,td->hd", mixed_low, middle_low, preferred_element_type=jnp.float32)
    grad_mixed = jnp.einsum("td,hd->th", middle_low, w_out, preferred_element_type=jnp.float32)
    grad_mixed = grad_mixed.astype(jnp.bfloat16).reshape(tok_rows, groups, repeat, HD)
    scores = attention_scores(query_low, key_all, mask_local, factor)
    probs = jnp.exp(scores - log_total)
    grad_probs = jnp.einsum(
        "tgrd,kgd->grtk", grad_mixed, value_all, preferred_element_type=jnp.float32
    )
    weighted = jnp.sum(probs * grad_probs, axis=-1, keepdims=True)
    grad_scores = (probs * (grad_probs - weighted)).astype(jnp.bfloat16)
    grad_turned = (
        jnp.einsum("grtk,kgd->tgrd", grad_scores, key_all, preferred_element_type=jnp.float32)
        * factor
    )
    grad_keyall = (
        jnp.einsum("grtk,tgrd->kgd", grad_scores, query_low, preferred_element_type=jnp.float32)
        * factor
    )
    grad_valueall = jnp.einsum(
        "grtk,tgrd->kgd", probs.astype(jnp.bfloat16), grad_mixed, preferred_element_type=jnp.float32
    )
    grad_keys, grad_values = (
        lax.psum_scatter(
            grad_keyall.reshape(total, groups * HD).astype(jnp.bfloat16),
            "wide",
            scatter_dimension=0,
            tiled=True,
        ).astype(jnp.float32),
        lax.psum_scatter(
            grad_valueall.reshape(total, groups * HD).astype(jnp.bfloat16),
            "wide",
            scatter_dimension=0,
            tiled=True,
        ).astype(jnp.float32),
    )
    grad_qraw, gain_q = pull_query(grad_turned.reshape(tok_rows, groups * repeat, HD))
    grad_kraw, gain_k = pull_key(grad_keys.reshape(tok_rows, groups, HD))
    query_back = grad_qraw.reshape(tok_rows, groups * repeat * HD).astype(jnp.bfloat16)
    key_back = grad_kraw.reshape(tok_rows, groups * HD).astype(jnp.bfloat16)
    value_back = grad_values.astype(jnp.bfloat16)
    grad_wquery = jnp.einsum(
        "td,th->dh", hidden_one, query_back, preferred_element_type=jnp.float32
    )
    grad_wkey = jnp.einsum("td,th->dh", hidden_one, key_back, preferred_element_type=jnp.float32)
    grad_wvalue = jnp.einsum(
        "td,th->dh", hidden_one, value_back, preferred_element_type=jnp.float32
    )
    partial_one = (
        jnp.einsum("th,dh->td", query_back, w_query, preferred_element_type=jnp.float32)
        + jnp.einsum("th,dh->td", key_back, w_key, preferred_element_type=jnp.float32)
        + jnp.einsum("th,dh->td", value_back, w_value, preferred_element_type=jnp.float32)
    )
    gain_one = jnp.sum(partial_one * unit_rows(input_float), axis=0)
    grad_input = (
        grad_middle
        + pull_one(lax.psum(partial_one.astype(jnp.bfloat16), "narrow").astype(jnp.float32))[0]
    )
    weight_grads = (
        grad_wquery,
        grad_wkey,
        grad_wvalue,
        grad_wout,
        grad_wgate,
        grad_wup,
        grad_wdown,
    )
    return (output_low, grad_input, weight_grads, (gain_one, gain_two, gain_q, gain_k))


def local(
    layer_input,
    grad_out,
    lengths,
    w_query,
    w_key,
    w_value,
    w_out,
    w_gate,
    w_up,
    w_down,
    gain_attn,
    gain_ffn,
    gain_query,
    gain_key,
):
    width = lax.axis_size("wide")
    shards = (w_query, w_key, w_value, w_out, w_gate, w_up, w_down)
    along_rows = (True, True, True, False, True, True, False)
    gains = (gain_attn, gain_ffn, gain_query, gain_key)
    totals = tuple(
        (
            jnp.zeros(
                (
                    (piece.shape[0] * width, piece.shape[1])
                    if rows_first
                    else (piece.shape[0], piece.shape[1] * width)
                ),
                jnp.float32,
            )
            for piece, rows_first in zip(shards, along_rows)
        )
    )
    gain_terms = tuple((jnp.zeros(gain.shape, jnp.float32) for gain in gains))
    outputs = []
    grad_inputs = []
    for micro in range(layer_input.shape[0]):
        gathered = (
            lax.all_gather(w_query, "wide", axis=0, tiled=True),
            lax.all_gather(w_key, "wide", axis=0, tiled=True),
            lax.all_gather(w_value, "wide", axis=0, tiled=True),
            lax.all_gather(w_out, "wide", axis=1, tiled=True),
            lax.all_gather(w_gate, "wide", axis=0, tiled=True),
            lax.all_gather(w_up, "wide", axis=0, tiled=True),
            lax.all_gather(w_down, "wide", axis=1, tiled=True),
        )
        output, grad_input, weight_grads, gain_grads = one_batch(
            layer_input[micro], grad_out[micro], lengths[micro], gathered, gains
        )
        outputs.append(output)
        grad_inputs.append(grad_input)
        gain_terms = tuple((running + fresh for running, fresh in zip(gain_terms, gain_grads)))
        totals = tuple((running + fresh for running, fresh in zip(totals, weight_grads)))
    results = (
        lax.psum_scatter(
            totals[0].astype(jnp.bfloat16), "wide", scatter_dimension=0, tiled=True
        ).astype(jnp.float32),
        lax.psum_scatter(
            totals[1].astype(jnp.bfloat16), "wide", scatter_dimension=0, tiled=True
        ).astype(jnp.float32),
        lax.psum_scatter(
            totals[2].astype(jnp.bfloat16), "wide", scatter_dimension=0, tiled=True
        ).astype(jnp.float32),
        lax.psum_scatter(
            totals[3].astype(jnp.bfloat16), "wide", scatter_dimension=1, tiled=True
        ).astype(jnp.float32),
        lax.psum_scatter(
            totals[4].astype(jnp.bfloat16), "wide", scatter_dimension=0, tiled=True
        ).astype(jnp.float32),
        lax.psum_scatter(
            totals[5].astype(jnp.bfloat16), "wide", scatter_dimension=0, tiled=True
        ).astype(jnp.float32),
        lax.psum_scatter(
            totals[6].astype(jnp.bfloat16), "wide", scatter_dimension=1, tiled=True
        ).astype(jnp.float32),
    )
    gain_total = lax.psum(gain_terms, ("wide", "narrow"))
    return (
        jnp.stack(outputs),
        jnp.stack(grad_inputs),
        results[0],
        results[1],
        results[2],
        results[3],
        results[4],
        results[5],
        results[6],
        gain_total[0],
        gain_total[1],
        gain_total[2],
        gain_total[3],
    )


def solution(mesh):
    in_specs = (
        P(None, "wide", None),
        P(None, "wide", None),
        P(),
        P("wide", "narrow"),
        P("wide", "narrow"),
        P("wide", "narrow"),
        P("narrow", "wide"),
        P("wide", "narrow"),
        P("wide", "narrow"),
        P("narrow", "wide"),
        P(),
        P(),
        P(),
        P(),
    )
    out_specs = (
        P(None, "wide", None),
        P(None, "wide", None),
        P("wide", "narrow"),
        P("wide", "narrow"),
        P("wide", "narrow"),
        P("narrow", "wide"),
        P("wide", "narrow"),
        P("wide", "narrow"),
        P("narrow", "wide"),
        P(),
        P(),
        P(),
        P(),
    )
    return jax.shard_map(local, mesh=mesh, in_specs=in_specs, out_specs=out_specs, check_vma=False)
```

profile of v0, /device:TPU:0, one launch (start us, length us, event | category | flops | bytes accessed | tf_op | source)
XLA Modules:
  0.0 1959.9 jit_solution(11782084816646856816)
XLA Ops:
  14.2 21.9 %all-gather.16.cloned.1.call-done = bf16[2048,256]{1,0:T(8,128)(2,1)} async-done(((bf16[256,256]{1,0:T(8,128)(2,1)}), bf16[2048,256]{1,0:T(8,128)(2,1)}) %all-gather.16.cloned.1.call-update) | async-done | bytes 1048592 | tf_op jit(solution)/shard_map/all_gather | solution.py:252
  39.5 21.7 %all-gather.20.cloned.1.call-done = bf16[2048,256]{1,0:T(8,128)(2,1)} async-done(((bf16[256,256]{1,0:T(8,128)(2,1)}), bf16[2048,256]{1,0:T(8,128)(2,1)}) %all-gather.20.cloned.1.call-update) | async-done | bytes 1048592 | tf_op jit(solution)/shard_map/all_gather | solution.py:251
  72.1 18.9 all-gather.24.cloned.1.call-done
  94.9 21.8 %all-gather.38.cloned.1.call-done = bf16[2048,256]{1,0:T(8,128)(2,1)} async-done(((bf16[256,256]{1,0:T(8,128)(2,1)}), bf16[2048,256]{1,0:T(8,128)(2,1)}) %all-gather.38.cloned.1.call-update) | async-done | bytes 1048592 | tf_op jit(solution)/shard_map/all_gather | solution.py:100
  122.2 20.3 %all-gather.40.cloned.1.call-done = bf16[2048,256]{0,1:T(8,128)(2,1)} async-done(((bf16[256,256]{0,1:T(8,128)(2,1)}), bf16[2048,256]{0,1:T(8,128)(2,1)}) %all-gather.40.cloned.1.call-update) | async-done | bytes 1048592 | tf_op jit(solution)/shard_map/all_gather | solution.py:99
  150.4 22.0 %all-gather.26.cloned.1.call-done = bf16[512,2048]{1,0:T(8,128)(2,1)} async-done(((bf16[512,256]{1,0:T(8,128)(2,1)}), bf16[512,2048]{1,0:T(8,128)(2,1)}) %all-gather.26.cloned.1.call-update) | async-done | bytes 2097168 | tf_op jit(solution)/shard_map/all_gather | solution.py:253
  175.8 52.0 %all-reduce.25.cloned.1.call-done = bf16[256,2048]{1,0:T(8,128)(2,1)} async-done(((bf16[256,2048]{1,0:T(8,128)(2,1)}), bf16[256,2048]{1,0:T(8,128)(2,1)}) %all-reduce.25.cloned.1.call-update) | async-done | bytes 1048592 | tf_op jit(solution)/shard_map/psum | solution.py:113
  262.1 20.3 %all-gather.18.cloned.1.call-done = bf16[2048,256]{1,0:T(8,128)(2,1)} async-done(((bf16[256,256]{1,0:T(8,128)(2,1)}), bf16[2048,256]{1,0:T(8,128)(2,1)}) %all-gather.18.cloned.1.call-update) | async-done | bytes 1048592 | tf_op jit(solution)/shard_map/all_gather | solution.py:100
  284.6 23.5 %all-gather.34.cloned.1.call-done = bf16[2048,256]{1,0:T(8,128)(2,1)} async-done(((bf16[256,256]{1,0:T(8,128)(2,1)}), bf16[2048,256]{1,0:T(8,128)(2,1)}) %all-gather.34.cloned.1.call-update) | async-done | bytes 1048592 | tf_op jit(solution)/shard_map/all_gather | solution.py:100
  310.6 23.4 %all-gather.44.cloned.1.call-done = bf16[2048,256]{0,1:T(8,128)(2,1)} async-done(((bf16[256,256]{0,1:T(8,128)(2,1)}), bf16[2048,256]{0,1:T(8,128)(2,1)}) %all-gather.44.cloned.1.call-update) | async-done | bytes 1048592 | tf_op jit(solution)/shard_map/all_gather | solution.py:99
  344.3 15.1 all-gather.22.cloned.1.call-done
  369.7 15.0 all-gather.36.cloned.1.call-done
  394.9 36.9 %all-gather.28.cloned.1.call-done = bf16[2048,1536]{1,0:T(8,128)(2,1)} async-done(((bf16[256,1536]{1,0:T(8,128)(2,1)}), bf16[2048,1536]{1,0:T(8,128)(2,1)}) %all-gather.28.cloned.1.call-update) | async-done | bytes 6291472 | tf_op jit(solution)/shard_map/all_gather | solution.py:254
  437.6 42.6 %all-gather.32.cloned.1.call-done = bf16[1536,2048]{1,0:T(8,128)(2,1)} async-done(((bf16[1536,256]{1,0:T(8,128)(2,1)}), bf16[1536,2048]{1,0:T(8,128)(2,1)}) %all-gather.32.cloned.1.call-update) | async-done | bytes 6291472 | tf_op jit(solution)/shard_map/all_gather | solution.py:256
  486.3 41.1 %all-gather.30.cloned.1.call-done = bf16[2048,1536]{1,0:T(8,128)(2,1)} async-done(((bf16[256,1536]{1,0:T(8,128)(2,1)}), bf16[2048,1536]{1,0:T(8,128)(2,1)}) %all-gather.30.cloned.1.call-update) | async-done | bytes 6291472 | tf_op jit(solution)/shard_map/all_gather | solution.py:255
  543.0 155.1 %all-reduce.31.cloned.1.call-done = (bf16[256,2048]{1,0:T(8,128)(2,1)}, bf16[256,2048]{1,0:T(8,128)(2,1)}, bf16[256,2048]{1,0:T(8,128)(2,1)}, bf16[256,2048]{1,0:T(8,128)(2,1)}) async-done(((bf16[256,2048]{1,0:T(8,128)(2,1)}, bf16[256,2048]{1,0:T(8,128)(2,1)}, bf16[256,2048]{1,0:T(8,128)(2,1)}, bf16[256,2048]{1,0:T(8,128)(2,1)}), (bf16[256,2048]{1,0:T(8,128)(2,1)}, bf16[256,2048]{1,0:T(8,128)(2,1)}, ...) | async-done | bytes 4194320 | tf_op jit(solution)/shard_map/psum | solution.py:113
  771.1 119.5 %all-reduce.29.cloned.1.call-done = (bf16[256,2048]{1,0:T(8,128)(2,1)}, bf16[256,2048]{1,0:T(8,128)(2,1)}, bf16[256,2048]{1,0:T(8,128)(2,1)}) async-done(((bf16[256,2048]{1,0:T(8,128)(2,1)}, bf16[256,2048]{1,0:T(8,128)(2,1)}, bf16[256,2048]{1,0:T(8,128)(2,1)}), (bf16[256,2048]{1,0:T(8,128)(2,1)}, bf16[256,2048]{1,0:T(8,128)(2,1)}, bf16[256,2048]{1,0:T(8,128)(2,1)})) %all-reduce.29.cloned.1.call-update) | async-done | bytes 3145744 | tf_op jit(solution)/shard_map/psum | solution.py:140
  1058.9 15.2 reduce-scatter.20.cloned.1.call-done
  1091.6 22.2 %reduce-scatter.18.cloned.1.call-done = bf16[256,256]{0,1:T(8,128)(2,1)} async-done(((bf16[2048,256]{0,1:T(8,128)(2,1)}), bf16[256,256]{0,1:T(8,128)(2,1)}) %reduce-scatter.18.cloned.1.call-update) | async-done | bytes 131088 | tf_op jit(solution)/shard_map/reduce_scatter | solution.py:171
  1116.9 35.9 %reduce-scatter.22.cloned.1.call-done = bf16[256,256]{0,1:T(8,128)(2,1)} async-done(((bf16[2048,256]{0,1:T(8,128)(2,1)}), bf16[256,256]{0,1:T(8,128)(2,1)}) %reduce-scatter.22.cloned.1.call-update) | async-done | bytes 131088 | tf_op jit(solution)/shard_map/reduce_scatter | solution.py:171
  1156.7 35.3 %reduce-scatter.26.cloned.1.call-done = bf16[256,256]{0,1:T(8,128)(2,1)} async-done(((bf16[2048,256]{0,1:T(8,128)(2,1)}), bf16[256,256]{0,1:T(8,128)(2,1)}) %reduce-scatter.26.cloned.1.call-update) | async-done | bytes 131088 | tf_op jit(solution)/shard_map/reduce_scatter | solution.py:171
  1195.9 35.7 %reduce-scatter.30.cloned.1.call-done = bf16[256,256]{0,1:T(8,128)(2,1)} async-done(((bf16[2048,256]{0,1:T(8,128)(2,1)}), bf16[256,256]{0,1:T(8,128)(2,1)}) %reduce-scatter.30.cloned.1.call-update) | async-done | bytes 131088 | tf_op jit(solution)/shard_map/reduce_scatter | solution.py:171
  1235.3 18.2 add_convert_fusion.2
  1253.8 8.0 fusion.401
  1274.7 17.4 add_convert_fusion.1
  1313.8 17.2 add_convert_fusion
  1372.6 27.2 %reduce-scatter.36.cloned.1.call-done = bf16[256,256]{1,0:T(8,128)(2,1)} async-done(((bf16[2048,256]{1,0:T(8,128)(2,1)}), bf16[256,256]{1,0:T(8,128)(2,1)}) %reduce-scatter.36.cloned.1.call-update) | async-done | bytes 131088 | tf_op jit(solution)/shard_map/reduce_scatter | solution.py:272
  1401.3 64.1 %reduce-scatter.40.cloned.1.call-done = bf16[256,1536]{1,0:T(8,128)(2,1)} async-done(((bf16[2048,1536]{1,0:T(8,128)(2,1)}), bf16[256,1536]{1,0:T(8,128)(2,1)}) %reduce-scatter.40.cloned.1.call-update) | async-done | bytes 786448 | tf_op jit(solution)/shard_map/reduce_scatter | solution.py:278
  1467.9 62.7 %reduce-scatter.42.cloned.1.call-done = bf16[256,1536]{1,0:T(8,128)(2,1)} async-done(((bf16[2048,1536]{1,0:T(8,128)(2,1)}), bf16[256,1536]{1,0:T(8,128)(2,1)}) %reduce-scatter.42.cloned.1.call-update) | async-done | bytes 786448 | tf_op jit(solution)/shard_map/reduce_scatter | solution.py:281
  1533.1 62.4 %reduce-scatter.44.cloned.1.call-done = bf16[1536,256]{1,0:T(8,128)(2,1)} async-done(((bf16[1536,2048]{1,0:T(8,128)(2,1)}), bf16[1536,256]{1,0:T(8,128)(2,1)}) %reduce-scatter.44.cloned.1.call-update) | async-done | bytes 786448 | tf_op jit(solution)/shard_map/reduce_scatter | solution.py:284
  1597.9 292.1 %all-reduce.27.cloned.1.call-done = (bf16[256,2048]{1,0:T(8,128)(2,1)}, bf16[256,2048]{1,0:T(8,128)(2,1)}, bf16[256,2048]{1,0:T(8,128)(2,1)}, bf16[256,2048]{1,0...) async-done(((bf16[256,2048]{1,0:T(8,128)(2,1)}, bf16[256,2048]{1,0:T(8,128)(2,1)}, ...) | async-done | bytes 8388624 | tf_op jit(solution)/shard_map/psum | solution.py:125
  1913.4 39.5 %all-reduce.16 = (f32[2048]{0:T(1024)}, f32[2048]{0:T(1024)}, f32[128]{0:T(128)}, f32[128]{0:T(128)}) all-reduce(f32[2048]{0:T(1024)S(1)} %add_add_fusion.17, f32[2048]{0:T(1024)S(1)} %add_add_fusion.16, f32[128]{0:T(128)S(1)} %add_add_fusion.19, f32[128]{0:T(128)S(1)} %add_add_fusion.18), channel_id=1, replica_groups=mesh['wide'=8,'narrow'=4] {'wide','narrow'}, use_global_device_ids=true, to_apply=%region_91.92 | all-reduce | flops 4352 | bytes 34816 | tf_op jit(solution)/shard_map/psum | solution.py:288
  (866 shorter events, 517.7 us)
Async XLA Ops:
  7.9 53.4 %all-gather.20.cloned.1.call-start = ((), (), s32[]{:S(2)}) async-start(), calls=%async_computation.17 | async-start | bytes 1179648 | tf_op jit(solution)/shard_map/all_gather | solution.py:251
  8.7 82.3 %all-gather.24.cloned.1.call-start = ((), (), s32[]{:S(2)}) async-start(), calls=%async_computation.19 | async-start | bytes 2359296 | tf_op jit(solution)/shard_map/all_gather | solution.py:250
  9.4 107.3 %all-gather.38.cloned.1.call-start = ((), (), s32[]{:S(2)}) async-start(), calls=%async_computation.26 | async-start | bytes 1179648 | tf_op jit(solution)/shard_map/all_gather | solution.py:100
  38.7 103.8 %all-gather.40.cloned.1.call-start = ((), (), s32[]{:S(2)}) async-start(), calls=%async_computation.27 | async-start | bytes 1179648 | tf_op jit(solution)/shard_map/all_gather | solution.py:99
  66.5 105.9 %all-gather.26.cloned.1.call-start = ((), (), s32[]{:S(2)}) async-start(), calls=%async_computation.20 | async-start | bytes 2359296 | tf_op jit(solution)/shard_map/all_gather | solution.py:253
  67.1 160.7 %all-reduce.25.cloned.1.call-start = ((), (), s32[]{:S(2)}) async-start(), calls=%async_computation.28 | async-start | bytes 2097152 | tf_op jit(solution)/shard_map/psum | solution.py:113
  175.7 83.9 %all-gather.42.cloned.1.call-start = ((), (), s32[]{:S(2)}) async-start(), calls=%async_computation.29 | async-start | bytes 1179648 | tf_op jit(solution)/shard_map/all_gather | solution.py:100
  236.4 71.7 %all-gather.34.cloned.1.call-start = ((), (), s32[]{:S(2)}) async-start(), calls=%async_computation.24 | async-start | bytes 1179648 | tf_op jit(solution)/shard_map/all_gather | solution.py:100
  241.8 92.3 %all-gather.44.cloned.1.call-start = ((), (), s32[]{:S(2)}) async-start(), calls=%async_computation.30 | async-start | bytes 1179648 | tf_op jit(solution)/shard_map/all_gather | solution.py:99
  246.6 112.7 %all-gather.22.cloned.1.call-start = ((), (), s32[]{:S(2)}) async-start(), calls=%async_computation.18 | async-start | bytes 1179648 | tf_op jit(solution)/shard_map/all_gather | solution.py:99
  247.9 136.8 %all-gather.36.cloned.1.call-start = ((), (), s32[]{:S(2)}) async-start(), calls=%async_computation.25 | async-start | bytes 1179648 | tf_op jit(solution)/shard_map/all_gather | solution.py:99
  249.2 182.7 %all-gather.28.cloned.1.call-start = ((), (), s32[]{:S(2)}) async-start(), calls=%async_computation.21 | async-start | bytes 7077888 | tf_op jit(solution)/shard_map/all_gather | solution.py:254
  249.8 230.4 %all-gather.32.cloned.1.call-start = ((), (), s32[]{:S(2)}) async-start(), calls=%async_computation.23 | async-start | bytes 7077888 | tf_op jit(solution)/shard_map/all_gather | solution.py:256
  250.4 277.0 %all-gather.30.cloned.1.call-start = ((), (), s32[]{:S(2)}) async-start(), calls=%async_computation.22 | async-start | bytes 7077888 | tf_op jit(solution)/shard_map/all_gather | solution.py:255
  250.9 447.2 %all-reduce.31.cloned.1.call-start = ((), (), s32[]{:S(2)}) async-start(), calls=%async_computation.48 | async-start | bytes 8388608 | tf_op jit(solution)/shard_map/psum | solution.py:113
  543.0 347.6 %all-reduce.29.cloned.1.call-start = ((), (), s32[]{:S(2)}) async-start(), calls=%async_computation.47 | async-start | bytes 6291456 | tf_op jit(solution)/shard_map/psum | solution.py:140
  770.3 278.2 %reduce-scatter.24.cloned.1.call-start = ((), (), s32[]{:S(2)}) async-start(), calls=%async_computation.35 | async-start | bytes 1179648 | tf_op jit(solution)/shard_map/reduce_scatter | solution.py:165
  920.9 129.3 %reduce-scatter.16.cloned.1.call-start = ((), (), s32[]{:S(2)}) async-start(), calls=%async_computation.31 | async-start | bytes 1179648 | tf_op jit(solution)/shard_map/reduce_scatter | solution.py:165
  942.0 109.8 %reduce-scatter.28.cloned.1.call-start = ((), (), s32[]{:S(2)}) async-start(), calls=%async_computation.37 | async-start | bytes 1179648 | tf_op jit(solution)/shard_map/reduce_scatter | solution.py:165
  959.1 114.9 %reduce-scatter.20.cloned.1.call-start = ((), (), s32[]{:S(2)}) async-start(), calls=%async_computation.33 | async-start | bytes 1179648 | tf_op jit(solution)/shard_map/reduce_scatter | solution.py:165
  969.3 144.5 %reduce-scatter.18.cloned.1.call-start = ((), (), s32[]{:S(2)}) async-start(), calls=%async_computation.32 | async-start | bytes 1179648 | tf_op jit(solution)/shard_map/reduce_scatter | solution.py:171
  980.6 172.2 %reduce-scatter.22.cloned.1.call-start = ((), (), s32[]{:S(2)}) async-start(), calls=%async_computation.34 | async-start | bytes 1179648 | tf_op jit(solution)/shard_map/reduce_scatter | solution.py:171
  991.4 200.6 %reduce-scatter.26.cloned.1.call-start = ((), (), s32[]{:S(2)}) async-start(), calls=%async_computation.36 | async-start | bytes 1179648 | tf_op jit(solution)/shard_map/reduce_scatter | solution.py:171
  1003.5 228.2 %reduce-scatter.30.cloned.1.call-start = ((), (), s32[]{:S(2)}) async-start(), calls=%async_computation.38 | async-start | bytes 1179648 | tf_op jit(solution)/shard_map/reduce_scatter | solution.py:171
  1017.4 349.8 %reduce-scatter.32.cloned.1.call-start = ((), (), s32[]{:S(2)}) async-start(), calls=%async_computation.39 | async-start | bytes 2359296 | tf_op jit(solution)/shard_map/reduce_scatter | solution.py:266
  1025.9 343.0 %reduce-scatter.38.cloned.1.call-start = ((), (), s32[]{:S(2)}) async-start(), calls=%async_computation.42 | async-start | bytes 2359296 | tf_op jit(solution)/shard_map/reduce_scatter | solution.py:275
  1048.4 322.5 %reduce-scatter.34.cloned.1.call-start = ((), (), s32[]{:S(2)}) async-start(), calls=%async_computation.40 | async-start | bytes 1179648 | tf_op jit(solution)/shard_map/reduce_scatter | solution.py:269
  1083.8 315.9 %reduce-scatter.36.cloned.1.call-start = ((), (), s32[]{:S(2)}) async-start(), calls=%async_computation.41 | async-start | bytes 1179648 | tf_op jit(solution)/shard_map/reduce_scatter | solution.py:272
  1235.2 230.3 %reduce-scatter.40.cloned.1.call-start = ((), (), s32[]{:S(2)}) async-start(), calls=%async_computation.43 | async-start | bytes 7077888 | tf_op jit(solution)/shard_map/reduce_scatter | solution.py:278
  1253.5 277.1 %reduce-scatter.42.cloned.1.call-start = ((), (), s32[]{:S(2)}) async-start(), calls=%async_computation.44 | async-start | bytes 7077888 | tf_op jit(solution)/shard_map/reduce_scatter | solution.py:281
  1292.1 303.4 %reduce-scatter.44.cloned.1.call-start = ((), (), s32[]{:S(2)}) async-start(), calls=%async_computation.45 | async-start | bytes 7077888 | tf_op jit(solution)/shard_map/reduce_scatter | solution.py:284
  1331.0 558.9 %all-reduce.27.cloned.1.call-start = ((), (), s32[]{:S(2)}) async-start(), calls=%async_computation.46 | async-start | bytes 16777216 | tf_op jit(solution)/shard_map/psum | solution.py:125
  (267 other events, 2897.5 us)
Sparse Core Ops, SparseCore 0:
  9.9 26.0 all-gather.15
  63.2 27.7 all-gather.23
  93.3 23.3 all-gather.37
  119.0 23.4 all-gather.39
  144.3 28.0 all-gather.25
  175.8 51.8 all-reduce.24
  259.0 23.3 all-gather.17
  284.7 23.3 all-gather.33
  310.6 23.4 all-gather.43
  335.8 23.4 all-gather.21
  361.2 23.4 all-gather.35
  386.4 45.3 all-gather.27
  433.6 46.5 all-gather.31
  481.9 45.3 all-gather.29
  543.1 155.0 all-reduce.30
  770.4 120.0 all-reduce.28
  921.0 35.0 reduce-scatter.23
  959.6 35.9 reduce-scatter.15
  998.9 35.9 reduce-scatter.27
  1038.0 35.9 reduce-scatter.19
  1077.8 35.9 reduce-scatter.17
  1116.8 35.9 reduce-scatter.21
  1156.0 35.9 reduce-scatter.25
  1195.6 35.9 reduce-scatter.29
  1234.7 41.1 reduce-scatter.31
  1279.2 41.0 reduce-scatter.37
  1324.1 35.9 reduce-scatter.33
  1363.7 35.9 reduce-scatter.35
  1403.7 61.7 reduce-scatter.39
  1468.9 61.6 reduce-scatter.41
  1533.8 61.6 reduce-scatter.43
  1598.9 290.9 all-reduce.26
  (2 shorter events, 45.9 us)
where the time goes:
time: 1970 us; the launch traced here: 1960 us
  waiting for transfers between devices  1330 us (68%)
  matrix products  388 us (20%)
  other arithmetic  128 us (6%)
  local copies, waits for them, and re-layouts  54.6 us (3%)
  blocking collectives  39.5 us (2%)
    psum x1, waiting for transfers between devices, one_batch(): lax.psum(ffn_part.astype(jnp.bfloat16), 'narrow').astype(jnp.float32)  292 us
    psum x2, waiting for transfers between devices, one_batch(): lax.psum(attn_part.astype(jnp.bfloat16), 'narrow').astype(jnp.float32)  207 us
    reduce_scatter x4, waiting for transfers between devices, one_batch(): lax.psum_scatter(grad_valueall.reshape(total, groups * HD).astype(jnp.bfl...  129 us
    psum x1, waiting for transfers between devices, one_batch(): lax.psum(partial_two.astype(jnp.bfloat16), 'narrow').astype(jnp.float32)  119 us
    all_gather x4, waiting for transfers between devices, one_batch(): lax.all_gather(key_low, 'wide', axis=0, tiled=True)  73.8 us
    all_gather x4, waiting for transfers between devices, one_batch(): lax.all_gather(value_low, 'wide', axis=0, tiled=True)  65.7 us
    reduce_scatter x1, waiting for transfers between devices, local(): lax.psum_scatter(totals[4].astype(jnp.bfloat16), 'wide', scatter_dimensio...  64.1 us
    reduce_scatter x1, waiting for transfers between devices, local(): lax.psum_scatter(totals[5].astype(jnp.bfloat16), 'wide', scatter_dimensio...  62.7 us
  transfers between devices with their start and end apart: 34, of which 28 were waited for; matrix products, arithmetic and copies ran while one was open for 20% of the time, Pallas kernels for 0%

commit v1 on v0

v1 whole, which is shorter than its diff:
```python
import functools
import math

import jax
import jax.numpy as jnp
from jax import lax
from jax.experimental import pallas as pl
from jax.experimental.pallas import tpu as pltpu
from jax.sharding import PartitionSpec as P

HD = 128
NDOC = 8

EPSILON = 1e-06
THETA = 1000000.0
FACTOR = 1.0 / math.sqrt(HD)
NEVER = -1e30
MESH = pl.DeviceIdType.MESH
LINE = 4
CHUNKS = 32


def rms_norm(values, gain):
    return values * lax.rsqrt(jnp.mean(values * values, axis=-1, keepdims=True) + EPSILON) * gain


def unit_rows(values):
    return values * lax.rsqrt(jnp.mean(values * values, axis=-1, keepdims=True) + EPSILON)


def rotate(values, cosine, sine):
    midway = values.shape[-1] // 2
    turned = jnp.concatenate([-values[..., midway:], values[..., :midway]], axis=-1)
    return values * cosine + turned * sine


def layout(lengths_row, total):
    finish = jnp.cumsum(lengths_row)
    starts = finish - lengths_row
    places = jnp.arange(total, dtype=jnp.int32)
    segment = jnp.sum((places[:, None] >= finish[None, :]).astype(jnp.int32), axis=1)
    member = segment[:, None] == jnp.arange(finish.shape[0], dtype=jnp.int32)[None, :]
    opening = jnp.sum(jnp.where(member, starts[None, :], 0), axis=1)
    return (segment, opening)


def angles(place):
    frequency = jnp.exp(-math.log(THETA) * jnp.arange(0, HD, 2).astype(jnp.float32) / HD)
    turning = place.astype(jnp.float32)[:, None] * frequency[None, :]
    turning = jnp.concatenate([turning, turning], axis=-1)
    return (jnp.cos(turning), jnp.sin(turning))


def tree_kernel(chunks, part, total, got_a, sum_a, got_b, a_send, a_recv, b_send, b_recv, c_send, c_recv):
    me = lax.axis_index("narrow")
    outer = (me == 0) | (me == LINE - 1)
    mate = jnp.where(me < 2, 1 - me, 5 - me)
    cross = LINE - 1 - me
    rows = part.shape[0] // chunks
    barrier = pltpu.get_barrier_semaphore()
    pl.semaphore_signal(barrier, 1, device_id={"narrow": mate}, device_id_type=MESH)

    def span(c):
        return pl.ds(pl.multiple_of(c * rows, rows), rows)

    def copy_a(c):
        return pltpu.make_async_remote_copy(
            part.at[span(c)], got_a.at[span(c)], a_send.at[c], a_recv.at[c],
            device_id={"narrow": mate}, device_id_type=MESH,
        )

    def copy_b(c):
        return pltpu.make_async_remote_copy(
            sum_a.at[span(c)], got_b.at[span(c)], b_send.at[c], b_recv.at[c],
            device_id={"narrow": cross}, device_id_type=MESH,
        )

    def copy_c(c):
        return pltpu.make_async_remote_copy(
            total.at[span(c)], total.at[span(c)], c_send.at[c], c_recv.at[c],
            device_id={"narrow": mate}, device_id_type=MESH,
        )

    @pl.when(outer)
    def _():
        pl.semaphore_wait(barrier, 1)

        @pl.loop(0, chunks)
        def _(c):
            copy_a(c).start()

        @pl.loop(0, chunks)
        def _(c):
            copy_a(c).wait_send()
            copy_c(c).wait_recv()

    @pl.when(jnp.logical_not(outer))
    def _():
        pl.semaphore_signal(barrier, 1, device_id={"narrow": cross}, device_id_type=MESH)
        pl.semaphore_wait(barrier, 2)

        def add(c):
            copy_a(c).wait_recv()
            sum_a[span(c)] = (
                part[span(c)].astype(jnp.float32) + got_a[span(c)].astype(jnp.float32)
            ).astype(jnp.bfloat16)

        def finish(c):
            copy_b(c).wait_recv()
            total[span(c)] = (
                sum_a[span(c)].astype(jnp.float32) + got_b[span(c)].astype(jnp.float32)
            ).astype(jnp.bfloat16)

        add(0)
        copy_b(0).start()

        @pl.loop(1, chunks)
        def _(c):
            add(c)
            copy_b(c).start()
            finish(c - 1)
            copy_c(c - 1).start()

        finish(chunks - 1)
        copy_c(chunks - 1).start()

        @pl.loop(0, chunks)
        def _(c):
            copy_b(c).wait_send()
            copy_c(c).wait_send()


def narrow_sum(part):
    if lax.axis_size("narrow") != LINE:
        return lax.psum(part, "narrow")
    rows, width = part.shape
    buffer = pltpu.VMEM((rows, width), jnp.bfloat16)
    semaphores = pltpu.SemaphoreType.DMA((CHUNKS,))
    return pl.pallas_call(
        functools.partial(tree_kernel, CHUNKS),
        out_shape=jax.ShapeDtypeStruct((rows, width), jnp.bfloat16),
        in_specs=[pl.BlockSpec(memory_space=pltpu.VMEM)],
        out_specs=pl.BlockSpec(memory_space=pltpu.VMEM),
        scratch_shapes=[buffer] * 3 + [semaphores] * 6,
        compiler_params=pltpu.CompilerParams(
            collective_id=0, has_side_effects=True, vmem_limit_bytes=40 << 20
        ),
        cost_estimate=pl.CostEstimate(flops=0, bytes_accessed=300_000_000, transcendentals=0),
        name="narrow_sum",
    )(part)


def contract(a, b, dims):
    return lax.dot_general(a, b, (dims, ((), ())), preferred_element_type=jnp.float32)


def attend_kernel(scalars, q_ref, k_ref, v_ref, qseg_ref, kseg_ref, o_ref, lse_ref, high, below, acc):
    own = scalars[0]
    first = scalars[1 + pl.program_id(0)]
    rows = q_ref.shape[1]
    pair = jnp.concatenate([q_ref[0, :, :HD], q_ref[0, :, HD:]], axis=0)
    qseg = jnp.concatenate([qseg_ref[0], qseg_ref[0]], axis=0)

    def raw(j):
        scores = contract(pair, k_ref[j, 0], ((1,), (1,)))
        return jnp.where(qseg == kseg_ref[0, j], scores, NEVER)

    scores = raw(own)
    upto = lax.broadcasted_iota(jnp.int32, (rows, rows), 1) <= lax.broadcasted_iota(
        jnp.int32, (rows, rows), 0
    )
    upto = jnp.concatenate([upto.astype(jnp.int32)] * 2, axis=0) != 0
    scores = jnp.where(upto, scores, NEVER)
    highest = jnp.max(scores, axis=1, keepdims=True)
    weight = jnp.exp((scores - highest) * FACTOR)
    high[...] = highest
    below[...] = jnp.sum(weight, axis=1, keepdims=True)
    acc[...] = contract(weight.astype(jnp.bfloat16), v_ref[own, 0], ((1,), (0,)))

    @pl.loop(first, own)
    def _(j):
        scores = raw(j)
        before = high[...]
        highest = jnp.maximum(before, jnp.max(scores, axis=1, keepdims=True))
        keep = jnp.exp((before - highest) * FACTOR)
        weight = jnp.exp((scores - highest) * FACTOR)
        high[...] = highest
        below[...] = below[...] * keep + jnp.sum(weight, axis=1, keepdims=True)
        acc[...] = acc[...] * keep + contract(weight.astype(jnp.bfloat16), v_ref[j, 0], ((1,), (0,)))

    mixed = (acc[...] / below[...]).astype(jnp.bfloat16)
    o_ref[0, :, :HD] = mixed[:rows]
    o_ref[0, :, HD:] = mixed[rows:]
    lse_ref[0, 0] = high[...] * FACTOR + jnp.log(below[...])


def attend(scalars, queries, keyvals, coded_own, coded):
    batch, rows, width = queries.shape
    blocks = keyvals.shape[0]
    groups = width // (2 * HD)
    return pl.pallas_call(
        attend_kernel,
        grid_spec=pltpu.PrefetchScalarGridSpec(
            num_scalar_prefetch=1,
            grid=(batch, groups),
            in_specs=[
                pl.BlockSpec((1, rows, 2 * HD), lambda m, g, s: (m, 0, g)),
                pl.BlockSpec((blocks, 1, rows, HD), lambda m, g, s: (0, m, 0, g)),
                pl.BlockSpec((blocks, 1, rows, HD), lambda m, g, s: (0, m, 0, groups + g)),
                pl.BlockSpec((1, rows, 1), lambda m, g, s: (m, 0, 0)),
                pl.BlockSpec((1, blocks, 1, rows), lambda m, g, s: (m, 0, 0, 0)),
            ],
            out_specs=[
                pl.BlockSpec((1, rows, 2 * HD), lambda m, g, s: (m, 0, g)),
                pl.BlockSpec((1, 1, 2 * rows, 1), lambda m, g, s: (m, g, 0, 0)),
            ],
            scratch_shapes=[
                pltpu.VMEM((2 * rows, 1), jnp.float32),
                pltpu.VMEM((2 * rows, 1), jnp.float32),
                pltpu.VMEM((2 * rows, HD), jnp.float32),
            ],
        ),
        out_shape=[
            jax.ShapeDtypeStruct((batch, rows, width), jnp.bfloat16),
            jax.ShapeDtypeStruct((batch, groups, 2 * rows, 1), jnp.float32),
        ],
        compiler_params=pltpu.CompilerParams(vmem_limit_bytes=48 << 20),
        cost_estimate=pl.CostEstimate(flops=4_000_000_000, bytes_accessed=12_000_000, transcendentals=4_000_000),
        name="attend",
    )(scalars, queries, keyvals, keyvals, coded_own, coded)


def attend_back_kernel(
    scalars, q_ref, kv_ref, do_ref, lse_ref, delta_ref, qseg_ref, kseg_ref, dq_ref, dkv_ref, acc
):
    own = scalars[0]
    first = scalars[1 + pl.program_id(0)]
    rows = q_ref.shape[1]
    groups = q_ref.shape[2] // (2 * HD)
    upto = lax.broadcasted_iota(jnp.int32, (rows, rows), 0) <= lax.broadcasted_iota(
        jnp.int32, (rows, rows), 1
    )
    upto = jnp.concatenate([upto.astype(jnp.int32)] * 2, axis=1) != 0
    qseg = qseg_ref[0]
    dkv_ref[...] = jnp.zeros_like(dkv_ref)
    for g in range(groups):
        left = 2 * g * HD
        pair = jnp.concatenate(
            [q_ref[0, :, left : left + HD], q_ref[0, :, left + HD : left + 2 * HD]], axis=0
        )
        dpair = jnp.concatenate(
            [do_ref[0, :, left : left + HD], do_ref[0, :, left + HD : left + 2 * HD]], axis=0
        )
        lse = lse_ref[0, g]
        delta = delta_ref[0, g]
        kcol = slice(g * HD, (g + 1) * HD)
        vcol = slice((groups + g) * HD, (groups + g + 1) * HD)

        def one(j, diagonal):
            keys = kv_ref[j, 0, :, kcol]
            scores = contract(keys, pair, ((1,), (1,))) * FACTOR
            valid = kseg_ref[0, j] == qseg
            if diagonal:
                valid = valid & upto
            probs = jnp.where(valid, jnp.exp(scores - lse), 0.0)
            dprobs = contract(kv_ref[j, 0, :, vcol], dpair, ((1,), (1,)))
            dscores = (probs * (dprobs - delta)).astype(jnp.bfloat16)
            dkv_ref[j, 0, :, kcol] = (contract(dscores, pair, ((1,), (0,))) * FACTOR).astype(jnp.bfloat16)
            dkv_ref[j, 0, :, vcol] = contract(probs.astype(jnp.bfloat16), dpair, ((1,), (0,))).astype(
                jnp.bfloat16
            )
            return contract(dscores, keys, ((0,), (0,)))

        acc[...] = one(own, True)

        @pl.loop(first, own)
        def _(j):
            acc[...] += one(j, False)

        dq_ref[0, :, left : left + HD] = acc[:rows] * FACTOR
        dq_ref[0, :, left + HD : left + 2 * HD] = acc[rows:] * FACTOR


def attend_back(scalars, queries, keyvals, grad_mixed, lse, delta, coded_own, coded):
    batch, rows, width = queries.shape
    blocks = keyvals.shape[0]
    groups = width // (2 * HD)
    row_spec = pl.BlockSpec((1, rows, width), lambda m, s: (m, 0, 0))
    all_spec = pl.BlockSpec((blocks, 1, rows, width), lambda m, s: (0, m, 0, 0))
    stat_spec = pl.BlockSpec((1, groups, 1, 2 * rows), lambda m, s: (m, 0, 0, 0))
    return pl.pallas_call(
        attend_back_kernel,
        grid_spec=pltpu.PrefetchScalarGridSpec(
            num_scalar_prefetch=1,
            grid=(batch,),
            in_specs=[
                row_spec,
                all_spec,
                row_spec,
                stat_spec,
                stat_spec,
                pl.BlockSpec((1, 1, 2 * rows), lambda m, s: (m, 0, 0)),
                pl.BlockSpec((1, blocks, rows, 1), lambda m, s: (m, 0, 0, 0)),
            ],
            out_specs=[row_spec, all_spec],
            scratch_shapes=[pltpu.VMEM((2 * rows, HD), jnp.float32)],
        ),
        out_shape=[
            jax.ShapeDtypeStruct((batch, rows, width), jnp.float32),
            jax.ShapeDtypeStruct((blocks, batch, rows, width), jnp.bfloat16),
        ],
        compiler_params=pltpu.CompilerParams(vmem_limit_bytes=56 << 20),
        cost_estimate=pl.CostEstimate(flops=10_000_000_000, bytes_accessed=24_000_000, transcendentals=4_000_000),
        name="attend_back",
    )(scalars, queries, keyvals, grad_mixed, lse, delta, coded_own, coded)


def gather_rows(shard):
    return lax.all_gather(shard, "wide", axis=0, tiled=True)


def scatter_rows(full):
    return lax.psum_scatter(
        full.astype(jnp.bfloat16), "wide", scatter_dimension=0, tiled=True
    ).astype(jnp.float32)


def scatter_columns(full):
    return lax.psum_scatter(
        full.astype(jnp.bfloat16), "wide", scatter_dimension=1, tiled=True
    ).astype(jnp.float32)


def local(
    layer_input,
    grad_out,
    lengths,
    w_query,
    w_key,
    w_value,
    w_out,
    w_gate,
    w_up,
    w_down,
    gain_attn,
    gain_ffn,
    gain_query,
    gain_key,
):
    batch, tok_rows, model = layer_input.shape
    width = lax.axis_size("wide")
    total = tok_rows * width
    rows = batch * tok_rows
    q_width, k_width, ffn = w_query.shape[1], w_key.shape[1], w_gate.shape[1]
    groups = k_width // HD
    own = lax.axis_index("wide")
    first_row = own * tok_rows
    low = jnp.bfloat16

    w_qkv = gather_rows(jnp.concatenate([w_query, w_key, w_value], axis=1))
    w_out_all = lax.all_gather(w_out, "wide", axis=1, tiled=True)

    segment, opening = jax.vmap(lambda one: layout(one, total))(lengths)
    positions = jnp.arange(total, dtype=jnp.int32)
    coded = jnp.where(segment == NDOC - 1, NDOC + positions[None, :], segment)
    coded_own = lax.dynamic_slice_in_dim(coded, first_row, tok_rows, axis=1)
    opening_own = lax.dynamic_slice_in_dim(opening, first_row, tok_rows, axis=1)
    padded = coded_own[:, 0] >= NDOC
    first = jnp.where(padded, own, opening_own[:, 0] // tok_rows)
    scalars = jnp.concatenate([own[None].astype(jnp.int32), first.astype(jnp.int32)])
    place = (first_row + jnp.arange(tok_rows, dtype=jnp.int32))[None, :] - opening_own
    cosine, sine = angles(place.reshape(rows))

    def head_norm(values, gain):
        return rotate(rms_norm(values, gain), cosine[:, None, :], sine[:, None, :])

    input_float = layer_input.reshape(rows, model).astype(jnp.float32)
    grad_low = grad_out.reshape(rows, model)
    normed_one, pull_one = jax.vjp(lambda values: rms_norm(values, gain_attn), input_float)
    hidden_one = normed_one.astype(low)
    qkv = contract(hidden_one, w_qkv, ((1,), (0,)))
    query_raw = qkv[:, :q_width].reshape(rows, q_width // HD, HD)
    key_raw = qkv[:, q_width : q_width + k_width].reshape(rows, groups, HD)
    value_low = qkv[:, q_width + k_width :].astype(low)
    query_turned, pull_query = jax.vjp(head_norm, query_raw, gain_query)
    key_turned, pull_key = jax.vjp(head_norm, key_raw, gain_key)
    query_low = query_turned.astype(low).reshape(batch, tok_rows, q_width)
    key_low = key_turned.astype(low).reshape(rows, k_width)
    keyvals = jnp.concatenate([key_low, value_low], axis=1).reshape(batch, tok_rows, 2 * k_width)
    keyvals = lax.all_gather(keyvals, "wide", axis=0, tiled=False)

    w_gate_up = gather_rows(jnp.concatenate([w_gate, w_up], axis=1))
    w_down_all = lax.all_gather(w_down, "wide", axis=1, tiled=True)

    coded_blocks = coded.reshape(batch, width, tok_rows)
    mixed_low, lse = attend(
        scalars, query_low, keyvals, coded_own[:, :, None], coded_blocks[:, :, None, :]
    )
    mixed_flat = mixed_low.reshape(rows, q_width)
    attn_part = contract(mixed_flat, w_out_all, ((1,), (0,))).astype(low)
    middle = input_float + narrow_sum(attn_part).astype(jnp.float32)
    normed_two, pull_two = jax.vjp(lambda values: rms_norm(values, gain_ffn), middle)
    hidden_two = normed_two.astype(low)

    gate_up = contract(hidden_two, w_gate_up, ((1,), (0,)))
    gate, up_proj = gate_up[:, :ffn], gate_up[:, ffn:]
    grad_active = contract(grad_low, w_down_all, ((1,), (1,)))
    active, pull_active = jax.vjp(lambda g, u: jax.nn.silu(g) * u, gate, up_proj)
    active_low = active.astype(low)
    grad_gate, grad_upper = pull_active(grad_active)
    ffn_back = jnp.concatenate([grad_gate.astype(low), grad_upper.astype(low)], axis=1)
    partial_two = contract(ffn_back, w_gate_up, ((1,), (1,)))
    gain_two = jnp.sum(partial_two * unit_rows(middle), axis=0)
    ffn_part = contract(active_low, w_down_all, ((1,), (0,))).astype(low)
    grad_wgate_up = scatter_rows(contract(hidden_two, ffn_back, ((0,), (0,))))
    grad_wdown = scatter_columns(contract(active_low, grad_low, ((0,), (0,))))

    grad_middle = grad_low.astype(jnp.float32) + pull_two(
        narrow_sum(partial_two.astype(low)).astype(jnp.float32)
    )[0]
    middle_low = grad_middle.astype(low)
    grad_mixed = contract(middle_low, w_out_all, ((1,), (1,)))
    grad_mixed = grad_mixed.astype(low)
    grad_wout = scatter_columns(contract(mixed_flat, middle_low, ((0,), (0,))))
    heads = q_width // HD
    delta = jnp.sum(
        (grad_mixed.astype(jnp.float32) * mixed_flat.astype(jnp.float32)).reshape(
            batch, tok_rows, heads, HD
        ),
        axis=-1,
    )
    delta = delta.transpose(0, 2, 1).reshape(batch, groups, 1, 2 * tok_rows)
    coded_pair = jnp.concatenate([coded_own, coded_own], axis=1)[:, None, :]
    grad_turned, grad_keyvals = attend_back(
        scalars,
        query_low,
        keyvals,
        grad_mixed.reshape(batch, tok_rows, q_width),
        lse.reshape(batch, groups, 1, 2 * tok_rows),
        delta,
        coded_pair,
        coded_blocks[:, :, :, None],
    )
    grad_keyvals = lax.psum_scatter(grad_keyvals, "wide", scatter_dimension=0, tiled=False)
    grad_keyvals = grad_keyvals.reshape(rows, 2 * k_width)
    grad_keys = grad_keyvals[:, :k_width].astype(jnp.float32)
    value_back = grad_keyvals[:, k_width:]

    output = (middle + narrow_sum(ffn_part).astype(jnp.float32)).astype(low)

    grad_qraw, gain_q = pull_query(grad_turned.reshape(rows, heads, HD))
    grad_kraw, gain_k = pull_key(grad_keys.reshape(rows, groups, HD))
    back = jnp.concatenate(
        [
            grad_qraw.reshape(rows, q_width).astype(low),
            grad_kraw.reshape(rows, k_width).astype(low),
            value_back,
        ],
        axis=1,
    )
    partial_one = contract(back, w_qkv, ((1,), (1,)))
    gain_one = jnp.sum(partial_one * unit_rows(input_float), axis=0)
    grad_wqkv = scatter_rows(contract(hidden_one, back, ((0,), (0,))))
    gain_total = lax.psum((gain_one, gain_two, gain_q, gain_k), ("wide", "narrow"))
    grad_input = (
        grad_middle + pull_one(narrow_sum(partial_one.astype(low)).astype(jnp.float32))[0]
    )
    return (
        output.reshape(batch, tok_rows, model),
        grad_input.reshape(batch, tok_rows, model),
        grad_wqkv[:, :q_width],
        grad_wqkv[:, q_width : q_width + k_width],
        grad_wqkv[:, q_width + k_width :],
        grad_wout,
        grad_wgate_up[:, :ffn],
        grad_wgate_up[:, ffn:],
        grad_wdown,
    ) + gain_total


def solution(mesh):
    in_specs = (
        P(None, "wide", None),
        P(None, "wide", None),
        P(),
        P("wide", "narrow"),
        P("wide", "narrow"),
        P("wide", "narrow"),
        P("narrow", "wide"),
        P("wide", "narrow"),
        P("wide", "narrow"),
        P("narrow", "wide"),
        P(),
        P(),
        P(),
        P(),
    )
    out_specs = (
        P(None, "wide", None),
        P(None, "wide", None),
        P("wide", "narrow"),
        P("wide", "narrow"),
        P("wide", "narrow"),
        P("narrow", "wide"),
        P("wide", "narrow"),
        P("wide", "narrow"),
        P("narrow", "wide"),
        P(),
        P(),
        P(),
        P(),
    )
    return jax.shard_map(local, mesh=mesh, in_specs=in_specs, out_specs=out_specs, check_vma=False)
```

time: 1970 us -> 966 us (0.49)
  waiting for transfers between devices: 1330 us -> 149 us
  Pallas kernels: 0 us -> 434 us
  matrix products: 388 us -> 136 us
    psum x4 -> x0, waiting for transfers between devices: 619 us -> none  [the longest x1 292 us: one_batch(): lax.psum(ffn_part.astype(jnp.bfloat16), 'narrow').astype(jnp.float32)]
    pallas_call x0 -> x6, Pallas kernels: none -> 434 us  [the longest x4 413 us: narrow_sum(): pl.pallas_call(functools.partial(tree_kernel, CHUNKS), out_shape=jax.Shap...]
    all_gather x15 -> x5, waiting for transfers between devices: 345 us -> 59.6 us  [the longest x2 29.7 us: gather_rows(): return lax.all_gather(shard, 'wide', axis=0, tiled=True)]
    reduce_scatter x15 -> x5, waiting for transfers between devices: 361 us -> 87.7 us  [the longest x2 49.5 us: scatter_columns(): lax.psum_scatter(full.astype(jnp.bfloat16), 'wide', scatter_dimension=1,...]
    dot_general x108 -> x12, matrix products: 388 us -> 136 us  [contract(): lax.dot_general(a, b, (dims, ((), ())), preferred_element_type=jnp.float32)]
    unnamed x530 -> x116, local copies, waits for them, and re-layouts: 37.2 us -> 10.9 us
    convert_element_type x27 -> x8, other arithmetic: 41.3 us -> 28 us  [the longest x1 5.94 us: local(): grad_qraw.reshape(rows, q_width).astype(low)]
  transfers between devices with their start and end apart: 34 -> 10, of which waited for: 28 -> 5; matrix products, arithmetic and copies ran while one was open for 20% -> 21% of each run, Pallas kernels for 0% -> 23%
where the time goes in v1:
time: 966 us; the launch traced here: 956 us
  Pallas kernels  434 us (45%)
  waiting for transfers between devices  149 us (15%)
  matrix products  136 us (14%)
  other arithmetic  124 us (13%)
  local copies, waits for them, and re-layouts  58.7 us (6%)
  blocking collectives  37.9 us (4%)
  between operations  15.6 us (2%)
    pallas_call x4, Pallas kernels, narrow_sum(): pl.pallas_call(functools.partial(tree_kernel, CHUNKS), out_shape=jax.Shap...  413 us
    dot_general x12, matrix products, contract(): lax.dot_general(a, b, (dims, ((), ())), preferred_element_type=jnp.float32)  136 us
    reduce_scatter x2, waiting for transfers between devices, scatter_columns(): lax.psum_scatter(full.astype(jnp.bfloat16), 'wide', scatter_dimension=1,...  49.5 us
    reduce_scatter x1, waiting for transfers between devices, local(): lax.psum_scatter(grad_keyvals, 'wide', scatter_dimension=0, tiled=False)  38.2 us
    psum x1, blocking collectives, local(): lax.psum((gain_one, gain_two, gain_q, gain_k), ('wide', 'narrow'))  37.9 us
    all_gather x2, waiting for transfers between devices, gather_rows(): return lax.all_gather(shard, 'wide', axis=0, tiled=True)  29.7 us
    reduce_sum x2, other arithmetic, rms_norm(): values * lax.rsqrt(jnp.mean(values * values, axis=-1, keepdims=True) + EP...  22.4 us
  transfers between devices with their start and end apart: 10, of which 5 were waited for; matrix products, arithmetic and copies ran while one was open for 21% of the time, Pallas kernels for 23%

profile of v1, /device:TPU:0, one launch (start us, length us, event | category | flops | bytes accessed | tf_op | source)
XLA Modules:
  0.0 956.4 jit_solution(484441028869427724)
XLA Ops:
  20.1 29.7 %all-gather.6.cloned.1.call-done = bf16[2048,1024]{1,0:T(8,128)(2,1)} async-done(((bf16[256,1024]{1,0:T(8,128)(2,1)}), bf16[2048,1024]{1,0:T(8,128)(2,1)}) %all-gather.6.cloned.1.call-update) | async-done | bytes 4194320 | tf_op jit(solution)/shard_map/all_gather | solution.py:319
  49.8 7.5 fusion.41
  76.2 6.1 reduce_sum.188
  114.7 11.4 %all-gather.8.cloned.1.call-done.k_ref.v_ref.kv_ref = bf16[8,4,256,512]{3,2,1,0:T(8,128)(2,1)} async-done(((bf16[1,4,256,512]{3,2,1,0:T(8,128)(2,1)}), bf16[8,4,256,512]{3,2,1,0:T(8,128)(2,1)}) %all-gather.8.cloned.1.call-update) | async-done | bytes 8388624 | tf_op jit(solution)/shard_map/all_gather | solution.py:390
  127.1 9.6 %attend.1 = (bf16[4,256,512]{2,1,0:T(8,128)(2,1)S(1)}, f32[4,2,512,1]{3,2,1,0:T(8,128)S(1)}) custom-call(s32[5]{0:T(128)S(1)} %pad_add_fusion.3.scalars, bf16[4,256,512]{2,1,0:T(8,128)(2,1)S(1)} %add_convert_fusion.1.q_ref, bf16[8,4,256,512]{3,2,1,0:T(8,128)(2,1)} %all-gather.8.cloned.1.call-done.k_ref.v_ref.kv_ref, ...), custom_call_target="tpu_custom_call" | custom-call | flops 4000000000 | bytes 12000000 | tf_op jit(solution)/shard_map/attend/pallas_call | solution.py:201
  137.7 18.4 %all-gather.10.cloned.1.call-done = bf16[512,2048]{1,0:T(8,128)(2,1)} async-done(((bf16[512,256]{1,0:T(8,128)(2,1)}), bf16[512,2048]{1,0:T(8,128)(2,1)}) %all-gather.10.cloned.1.call-update) | async-done | bytes 2097168 | tf_op jit(solution)/shard_map/all_gather | solution.py:361
  156.1 4.3 convolution_convert_fusion.3.part
  160.4 104.9 %narrow_sum.4 = bf16[1024,2048]{1,0:T(8,128)(2,1)S(1)} custom-call(bf16[1024,2048]{1,0:T(8,128)(2,1)S(1)} %convolution_convert_fusion.3.part), custom_call_target="tpu_custom_call" | custom-call | bytes 300000000 | tf_op jit(solution)/shard_map/narrow_sum/pallas_call | solution.py:139
  271.3 18.9 %fusion.42 = f32[1024,3072]{1,0:T(8,128)} fusion(bf16[1024,2048]{1,0:T(8,128)(2,1)} %multiply_convert_fusion, bf16[2048,3072]{1,0:T(8,128)(2,1)} %all-gather.12.cloned.1.call-done), kind=kOutput, calls=%fused_computation.130 | convolution fusion | flops 12884901888 | bytes 29360128 | tf_op jit(solution)/shard_map/dot_general | solution.py:154
  290.2 17.0 %fusion.10 = (bf16[1024,1536]{1,0:T(8,128)(2,1)}, bf16[1024,1536]{1,0:T(8,128)(2,1)}, bf16[1024,1536]{1,0:T(8,128)(2,1)}) fusion(f32[1024,3072]{1,0:T(8,128)} %fusion.42, bf16[1024,2048]{1,0:T(8,128)(2,1)} %bitcast.105, bf16[1536,2048]{1,0:T(8,128)(2,1)} %all-gather.14.cloned.1.call-done), kind=kOutput, calls=%fused_computation.28 | convolution fusion | flops 6467616768 | bytes 32505856 | tf_op jit(solution)/shard_map/dot_general | solution.py:154
  307.2 20.9 %fusion.39 = (bf16[1024,2048]{1,0:T(8,128)(2,1)}, f32[1024,2048]{1,0:T(8,128)}) fusion(bf16[2048,3072]{1,0:T(8,128)(2,1)} %all-gather.12.cloned.1.call-done, bf16[1024,1536]{1,0:T(8,128)(2,1)} %get-tuple-element.36, bf16[1024,1536]{1,0:T(8,128)(2,1)} %get-tuple-element.35), kind=kOutput, calls=%fused_computation.127 | convolution fusion | flops 12899581952 | bytes 31457280 | tf_op jit(solution)/shard_map/dot_general | solution.py:154
  330.4 101.9 %narrow_sum.6 = bf16[1024,2048]{1,0:T(8,128)(2,1)S(1)} custom-call(bf16[1024,2048]{1,0:T(8,128)(2,1)S(1)} %copy-done.3), custom_call_target="tpu_custom_call" | custom-call | bytes 300000000 | tf_op jit(solution)/shard_map/narrow_sum/pallas_call | solution.py:139
  432.3 6.0 multiply_reduce_fusion
  438.3 8.3 convolution_convert_fusion.2.part
  446.6 101.3 %narrow_sum.5 = bf16[1024,2048]{1,0:T(8,128)(2,1)S(1)} custom-call(bf16[1024,2048]{1,0:T(8,128)(2,1)S(1)} %convolution_convert_fusion.2.part), custom_call_target="tpu_custom_call" | custom-call | bytes 300000000 | tf_op jit(solution)/shard_map/narrow_sum/pallas_call | solution.py:139
  548.0 11.8 %fusion = (f32[1024,2048]{1,0:T(8,128)}, bf16[1024,2048]{1,0:T(8,128)(2,1)}) fusion(bf16[1024,2048]{1,0:T(8,128)(2,1)S(1)} %narrow_sum.6, bf16[1024,2048]{1,0:T(8,128)(2,1)S(1)} %copy-done.1, bf16[4,256,2048]{2,1,0:T(8,128)(2,1)} %param.14, f32[1024]{0:T(1024)S(1)} %multiply_multiply_fusion.5, f32[2048]{0:T(1024)S(1)} %copy-done.44, f32[1024]{0:T(1024)S(1)} %fusion.28, ...), kind=kLoop, calls=%fused_computation.5 | loop fusion | flops 29360128 | bytes 33570816 | tf_op jit(solution)/shard_map/add | solution.py:418
  559.8 7.5 convert_multiply_fusion.3
  576.9 12.2 %attend_back.1 = (f32[4,256,512]{2,1,0:T(8,128)}, bf16[8,4,256,512]{3,2,1,0:T(8,128)(2,1)}) custom-call(s32[5]{0:T(128)} %copy-done.8, bf16[4,256,512]{2,1,0:T(8,128)(2,1)} %copy-done.4, bf16[8,4,256,512]{3,2,1,0:T(8,128)(2,1)} %all-gather.8.cloned.1.call-done.k_ref.v_ref.kv_ref, bf16[4,256,512]{2,1,0:T(8,128)(2,1)} %bitcast.122, ...), custom_call_target="tpu_custom_call" | custom-call | flops 10000000000 | bytes 24000000 | tf_op jit(solution)/shard_map/attend_back/pallas_call | solution.py:291
  589.2 7.1 convolution_convert_fusion.5
  596.4 11.5 %convolution_convert_fusion.1 = bf16[1536,2048]{1,0:T(8,128)(2,1)} fusion(bf16[1024,1536]{1,0:T(8,128)(2,1)} %get-tuple-element.37, bf16[1024,2048]{1,0:T(8,128)(2,1)} %bitcast.106), kind=kOutput, calls=%fused_computation.25 | convolution fusion | flops 6445596672 | bytes 13631488 | tf_op jit(solution)/shard_map/dot_general | solution.py:154
  615.1 5.9 multiply_reduce_fusion.3
  623.3 5.9 fusion.13
  630.4 38.2 %reduce-scatter.6.cloned.1.call-done = bf16[1,4,256,512]{3,2,1,0:T(8,128)(2,1)} async-done(((bf16[8,4,256,512]{3,2,1,0:T(8,128)(2,1)}), bf16[1,4,256,512]{3,2,1,0:T(8,128)(2,1)}) %reduce-scatter.6.cloned.1.call-update) | async-done | bytes 1048592 | tf_op jit(solution)/shard_map/reduce_scatter | solution.py:444
  677.3 16.5 %multiply_reduce_fusion.6 = (f32[128]{0:T(128)S(1)}, f32[1024,2]{1,0:T(8,128)S(1)}, f32[1024,2,128]{2,1,0:T(2,128)}) fusion(f32[1024,2,128]{2,1,0:T(2,128)S(1)} %copy-done.16, f32[1024,2]{1,0:T(8,128)S(1)} %copy-done.25, f32[128]{0:T(128)S(1)} %copy-done.52, f32[1024,2,64]{2,1,0:T(2,128)S(1)} %get-tuple-element.47, f32[1024,2,64]{2,1,0:T(2,128)S(1)} %get-tuple-element.46, ...), kind=kLoop, calls=%fused_computation.70 | loop fusion | flops 2357120 | bytes 4736000 | tf_op jit(solution)/shard_map/transpose(jvp())/reduce_sum | solution.py:24
  694.2 5.1 fusion.20
  699.5 6.7 convolution_convert_fusion.4
  706.3 20.3 %convolution_convert_fusion = bf16[2048,3072]{1,0:T(8,128)(2,1)} fusion(bf16[1024,2048]{1,0:T(8,128)(2,1)} %multiply_convert_fusion, bf16[1024,1536]{1,0:T(8,128)(2,1)} %get-tuple-element.36, bf16[1024,1536]{1,0:T(8,128)(2,1)} %get-tuple-element.35), kind=kOutput, calls=%fused_computation.3 | convolution fusion | flops 12903776256 | bytes 23068672 | tf_op jit(solution)/shard_map/dot_general | solution.py:154
  728.5 49.5 %reduce-scatter.14.cloned.1.call-done = bf16[1536,256]{1,0:T(8,128)(2,1)} async-done(((bf16[1536,2048]{1,0:T(8,128)(2,1)}), bf16[1536,256]{1,0:T(8,128)(2,1)}) %reduce-scatter.14.cloned.1.call-update) | async-done | bytes 786448 | tf_op jit(solution)/shard_map/reduce_scatter | solution.py:329
  780.4 6.4 fusion.40
  786.8 104.5 %narrow_sum.7 = bf16[1024,2048]{1,0:T(8,128)(2,1)S(1)} custom-call(bf16[1024,2048]{1,0:T(8,128)(2,1)S(1)} %get-tuple-element.60.part), custom_call_target="tpu_custom_call" | custom-call | bytes 300000000 | tf_op jit(solution)/shard_map/narrow_sum/pallas_call | solution.py:139
  894.7 37.9 %all-reduce.4 = (f32[2048]{0:T(1024)}, f32[2048]{0:T(1024)}, f32[128]{0:T(128)}, f32[128]{0:T(128)}) all-reduce(f32[2048]{0:T(1024)S(1)} %get-tuple-element.25, f32[2048]{0:T(1024)S(1)} %get-tuple-element.21, f32[128]{0:T(128)S(1)} %get-tuple-element.23, ...), channel_id=1, replica_groups=mesh['wide'=8,'narrow'=4] {'wide','narrow'}, use_global_device_ids=true, to_apply=%region_18.19 | all-reduce | flops 4352 | bytes 34816 | tf_op jit(solution)/shard_map/psum | solution.py:464
  932.6 9.5 fusion.1
  (233 shorter events, 118.1 us)
Async XLA Ops:
  7.2 9.7 %copy-start.51 = (f32[128]{0:T(128)S(1)}, f32[128]{0:T(128)}, u32[]{:S(2)}) copy-start(f32[128]{0:T(128)} %param.27) | copy-start | bytes 1540
  7.2 9.8 %copy-start.40 = (f32[2048]{0:T(1024)S(1)}, f32[2048]{0:T(1024)}, u32[]{:S(2)}) copy-start(f32[2048]{0:T(1024)} %param.24) | copy-start | bytes 24580
  7.2 42.6 %all-gather.6.cloned.1.call-start = ((), (), s32[]{:S(2)}) async-start(), calls=%async_computation.5 | async-start | bytes 4718592 | tf_op jit(solution)/shard_map/all_gather | solution.py:319
  9.2 116.9 %all-gather.8.cloned.1.call-start = ((), (), s32[]{:S(2)}) async-start(), calls=%async_computation.6 | async-start | bytes 9437184 | tf_op jit(solution)/shard_map/all_gather | solution.py:390
  16.9 65.4 %copy-start.20 = (f32[1024,128]{1,0:T(8,128)}, f32[1024,128]{1,0:T(8,128)S(1)}, u32[]{:S(2)}) copy-start(f32[1024,128]{1,0:T(8,128)S(1)} %get-tuple-element.54) | copy-start | bytes 1572868
  16.9 85.4 %copy-start.26 = (f32[1024,128]{1,0:T(8,128)}, f32[1024,128]{1,0:T(8,128)S(1)}, u32[]{:S(2)}) copy-start(f32[1024,128]{1,0:T(8,128)S(1)} %get-tuple-element.55) | copy-start | bytes 1572868
  71.7 84.4 %all-gather.10.cloned.1.call-start = ((), (), s32[]{:S(2)}) async-start(), calls=%async_computation.7 | async-start | bytes 2359296 | tf_op jit(solution)/shard_map/all_gather | solution.py:361
  72.4 198.9 %all-gather.12.cloned.1.call-start = ((), (), s32[]{:S(2)}) async-start(), calls=%async_computation.8 | async-start | bytes 14155776 | tf_op jit(solution)/shard_map/all_gather | solution.py:319
  75.0 215.2 %all-gather.14.cloned.1.call-start = ((), (), s32[]{:S(2)}) async-start(), calls=%async_computation.9 | async-start | bytes 7077888 | tf_op jit(solution)/shard_map/all_gather | solution.py:393
  75.6 593.0 %reduce-scatter.6.cloned.1.call-start = ((), (), s32[]{:S(2)}) async-start(), calls=%async_computation.10 | async-start | bytes 9437184 | tf_op jit(solution)/shard_map/reduce_scatter | solution.py:444
  82.4 6.7 copy-start.49
  89.0 37.0 %copy-start.8 = (s32[5]{0:T(128)}, s32[5]{0:T(128)S(1)}, u32[]{:S(2)}) copy-start(s32[5]{0:T(128)S(1)} %pad_add_fusion.3.scalars) | copy-start | bytes 64
  98.6 6.8 copy-start.22
  114.6 22.1 %copy-start.4 = (bf16[4,256,512]{2,1,0:T(8,128)(2,1)}, bf16[4,256,512]{2,1,0:T(8,128)(2,1)S(1)}, u32[]{:S(2)}) copy-start(bf16[4,256,512]{2,1,0:T(8,128)(2,1)S(1)} %add_convert_fusion.1.q_ref) | copy-start | bytes 3145732
  160.4 104.9 %copy-start.10 = (bf16[4,256,2048]{2,1,0:T(8,128)(2,1)S(1)}, bf16[4,256,2048]{2,1,0:T(8,128)(2,1)}, u32[]{:S(2)}) copy-start(bf16[4,256,2048]{2,1,0:T(8,128)(2,1)} %param.14) | copy-start | bytes 12582916
  330.4 101.9 %copy-start.1 = (bf16[1024,2048]{1,0:T(8,128)(2,1)S(1)}, bf16[1024,2048]{1,0:T(8,128)(2,1)}, u32[]{:S(2)}) copy-start(bf16[1024,2048]{1,0:T(8,128)(2,1)} %copy-done) | copy-start | bytes 12582916
  330.4 101.9 %copy-start.11 = (bf16[4,256,2048]{2,1,0:T(8,128)(2,1)S(1)}, bf16[4,256,2048]{2,1,0:T(8,128)(2,1)}, u32[]{:S(2)}) copy-start(bf16[4,256,2048]{2,1,0:T(8,128)(2,1)} %param.14) | copy-start | bytes 12582916
  330.4 107.9 %slice-start = ((s8[6291456]{0:T(1024)(128)(4,1)}), s8[2097152]{0:T(1024)(128)(4,1)S(1)}, s32[]{:S(2)}) async-start(s8[6291456]{0:T(1024)(128)(4,1)} %bitcast.120), calls=%async_computation.15 | async-start | bytes 4194304
  548.0 11.9 %copy-start.7 = (bf16[4,256,512]{2,1,0:T(8,128)(2,1)S(1)}, bf16[4,256,512]{2,1,0:T(8,128)(2,1)}, u32[]{:S(2)}) copy-start(bf16[4,256,512]{2,1,0:T(8,128)(2,1)} %copy-done.6) | copy-start | bytes 3145732
  548.0 11.8 %copy-start.53 = (bf16[512,2048]{1,0:T(8,128)(2,1)S(1)}, bf16[512,2048]{1,0:T(8,128)(2,1)}, u32[]{:S(2)}) copy-start(bf16[512,2048]{1,0:T(8,128)(2,1)} %all-gather.10.cloned.1.call-done) | copy-start | bytes 6291460
  589.2 137.5 %reduce-scatter.10.cloned.1.call-start = ((), (), s32[]{:S(2)}) async-start(), calls=%async_computation.12 | async-start | bytes 2359296 | tf_op jit(solution)/shard_map/reduce_scatter | solution.py:329
  596.4 181.6 %reduce-scatter.14.cloned.1.call-start = ((), (), s32[]{:S(2)}) async-start(), calls=%async_computation.14 | async-start | bytes 7077888 | tf_op jit(solution)/shard_map/reduce_scatter | solution.py:329
  607.9 334.2 %reduce-scatter.8.cloned.1.call-start = ((), (), s32[]{:S(2)}) async-start(), calls=%async_computation.11 | async-start | bytes 4718592 | tf_op jit(solution)/shard_map/reduce_scatter | solution.py:323
  615.1 7.2 copy-start.39
  629.3 44.6 %copy-start.28 = (f32[1024,128]{1,0:T(8,128)S(1)}, f32[1024,128]{1,0:T(8,128)}, u32[]{:S(2)}) copy-start(f32[1024,128]{1,0:T(8,128)} %copy-done.26) | copy-start | bytes 1572868
  677.3 16.7 %copy-start.43 = (f32[1024,2]{0,1:T(2,128)S(1)}, f32[1024,2]{0,1:T(2,128)}, u32[]{:S(2)}) copy-start(f32[1024,2]{0,1:T(2,128)} %copy-done.42) | copy-start | bytes 24580
  706.2 239.4 %reduce-scatter.12.cloned.1.call-start = ((), (), s32[]{:S(2)}) async-start(), calls=%async_computation.13 | async-start | bytes 14155776 | tf_op jit(solution)/shard_map/reduce_scatter | solution.py:323
  726.6 53.8 %copy-start.37 = (bf16[1024,256]{1,0:T(8,128)(2,1)S(1)}, bf16[1024,256]{1,0:T(8,128)(2,1)}, u32[]{:S(2)}) copy-start(bf16[1024,256]{1,0:T(8,128)(2,1)} %get-tuple-element.49) | copy-start | bytes 1572868
  786.8 104.5 %copy-start.12 = (bf16[4,256,2048]{2,1,0:T(8,128)(2,1)S(1)}, bf16[4,256,2048]{2,1,0:T(8,128)(2,1)}, u32[]{:S(2)}) copy-start(bf16[4,256,2048]{2,1,0:T(8,128)(2,1)} %param.14) | copy-start | bytes 12582916
  786.8 104.5 %copy-start.41 = (f32[2048]{0:T(1024)S(1)}, f32[2048]{0:T(1024)}, u32[]{:S(2)}) copy-start(f32[2048]{0:T(1024)} %param.24) | copy-start | bytes 24580
  786.8 104.5 %copy-start.46 = (f32[1024]{0:T(1024)S(1)}, f32[1024]{0:T(1024)}, u32[]{:S(2)}) copy-start(f32[1024]{0:T(1024)} %copy-done.45) | copy-start | bytes 12292
  891.3 41.2 %copy-start.48 = (f32[1,2,4,128]{3,1,2,0:T(2,128)S(1)}, f32[1,2,4,128]{3,1,2,0:T(2,128)}, u32[]{:S(2)}) copy-start(f32[1,2,4,128]{3,1,2,0:T(2,128)} %copy-done.47) | copy-start | bytes 12292
  (34 other events, 131.7 us)
Sparse Core Ops, SparseCore 0:
  10.5 39.2 all-gather.5
  71.8 54.2 all-gather.7
  128.0 28.0 all-gather.9
  158.4 71.9 all-gather.11
  232.2 46.5 all-gather.13
  589.3 79.2 reduce-scatter.5
  671.9 41.0 reduce-scatter.9
  716.4 61.5 reduce-scatter.13
  781.4 51.1 reduce-scatter.7
  835.9 92.8 reduce-scatter.11
